TPU v7x, 32 devices: a whole 2x2x4 slice. The times are simulated.
32 devices in a mesh: enc: 8 (over z, x), tp: 4 (over y, core).
Axes of the slice: x: 2, y: 2, z: 4, core: 2. Of those that a mesh axis runs over, the one named last changes fastest.
Arguments:
- grad_rows: bfloat16 [3072, 8192], P('enc', 'tp'), may hold values from -6 to 6
- features: bfloat16 [3072, 1280], P('enc'), may hold values from -6 to 6
- block_in: bfloat16 [3072, 1280], P('enc', 'tp'), may hold values from -6 to 6
- patch_counts: int32 [8, 3], replicated, may hold values from 32 to 128, as said below
- owner: int32 [8, 3], replicated, may hold values from 0 to 7, as said below
- ln1_gain: float32 [1280], replicated, may hold values from 0.5 to 1.5
- w_qkv: bfloat16 [1280, 16, 240], P(None, 'tp')
- w_out: bfloat16 [1280, 1280], P('tp'), may hold values from -0.15625 to 0.15625
- w_proj: bfloat16 [1280, 8192], P(None, 'tp'), may hold values from -0.15625 to 0.15625
Outputs:
- grad_input: bfloat16 [3072, 1280], P('enc', 'tp')
- grad_proj: float32 [1280, 8192], P('enc', 'tp')
- grad_qkv: float32 [1280, 16, 240], P('enc', 'tp')
- grad_out: float32 [1280, 1280], P('tp', 'enc')
- grad_ln1: float32 [1280], P('enc')
Inputs may be any that keep to these rules, and one draw needn't show every extreme that they name: `patch_counts`: some image has exactly 128 live rows and some exactly 32. `owner`: each encoder device receives exactly 3 images, never two from the same block.
All inputs are finite; a program needn't handle non-finite values.
Results may differ from a plain program's by a relative error of at most 0.033.
Values may be sent and summed in bfloat16 or wider, within the bound.
A program may use at most 64 MiB of HBM per device.

v0:
```python
import jax
import jax.numpy as jnp
from jax import lax
from jax.sharding import PartitionSpec as P

TILE = 128
EPSILON = 1e-05


def shortened(shard):

    def short(part):
        return part.astype(jnp.bfloat16) if part.dtype == jnp.float32 else part

    return jax.tree.map(short, shard)


def normalize(values):
    centred = values - jnp.mean(values, axis=-1, keepdims=True)
    variance = jnp.mean(centred * centred, axis=-1, keepdims=True)
    inverse = lax.rsqrt(variance + EPSILON)
    return (centred * inverse, inverse)


def norm_back(incoming, normed, inverse, gain):
    scaled = incoming * gain
    inner_mean = jnp.mean(scaled * normed, axis=-1, keepdims=True)
    outgoing = inverse * (scaled - jnp.mean(scaled, axis=-1, keepdims=True) - normed * inner_mean)
    return (outgoing, jnp.sum(incoming * normed, axis=0))


def dot_nt(left, right):
    return lax.dot_general(
        left, right, (((1,), (1,)), ((), ())), preferred_element_type=jnp.float32
    )


def dot_tn(left, right):
    return lax.dot_general(
        left, right, (((0,), (0,)), ((), ())), preferred_element_type=jnp.float32
    )


def shards(grad_rows, features, block_in, patch_counts, owner, ln1_gain, w_qkv, w_out, w_proj):
    groups = lax.axis_size("enc")
    device = lax.axis_index("enc")
    tp_rank = lax.axis_index("tp")
    block_rows = grad_rows.shape[0]
    img_group = block_rows // TILE
    block_full = lax.all_gather(block_in, "tp", axis=1, tiled=True)
    line_index = jnp.arange(TILE, dtype=jnp.int32)
    peer_index = jnp.arange(groups, dtype=jnp.int32)
    own_counts = lax.dynamic_index_in_dim(patch_counts, device, 0, keepdims=False)
    own_owner = lax.dynamic_index_in_dim(owner, device, 0, keepdims=False)
    live_own = line_index[None, :] < own_counts[:, None]

    def outgoing(row_block):
        columns = row_block.shape[1]
        tiles = row_block.reshape(img_group, TILE, columns)
        tiles = jnp.where(live_own[:, :, None], tiles, jnp.zeros_like(tiles))
        return jnp.zeros((groups, TILE, columns), row_block.dtype).at[own_owner].set(tiles)

    sends = jnp.any(owner == device, axis=1)
    sends_int = sends.astype(jnp.int32)
    rank = jnp.cumsum(sends_int) - sends_int
    slot_index = jnp.arange(img_group, dtype=jnp.int32)
    source_of = jnp.sum(
        jnp.where(sends[None, :] & (rank[None, :] == slot_index[:, None]), peer_index[None, :], 0),
        axis=1,
    )
    source_owner = jnp.take(owner, source_of, axis=0)
    source_counts = jnp.take(patch_counts, source_of, axis=0)
    arrived_counts = jnp.sum(jnp.where(source_owner == device, source_counts, 0), axis=1)
    live_tiles = line_index[None, :] < arrived_counts[:, None]
    shared = lax.psum_scatter(
        dot_nt(grad_rows, w_proj).astype(jnp.bfloat16), "tp", scatter_dimension=1, tiled=True
    ).astype(jnp.float32)
    received = lax.all_to_all(
        outgoing(shared).astype(jnp.bfloat16), "enc", split_axis=0, concat_axis=0, tiled=True
    ).astype(jnp.float32)
    vis_grad = lax.all_gather(
        shortened(jnp.take(received, source_of, axis=0).reshape(block_rows, received.shape[2])),
        "tp",
        axis=1,
        tiled=True,
    )
    kept_rows = jnp.where(live_own.reshape(-1)[:, None], features, jnp.zeros_like(features))
    proj_term = dot_tn(kept_rows, grad_rows)
    features_dim = block_full.shape[1]
    heads_here = w_qkv.shape[1]
    head_size = w_qkv.shape[2] // 3
    rows_here = block_full.shape[0]
    qkv_flat = w_qkv.reshape(features_dim, heads_here * 3 * head_size)
    normed1, inverse1 = normalize(block_full.astype(jnp.float32))
    normed_in = (normed1 * ln1_gain).astype(jnp.bfloat16)
    packed = jnp.dot(normed_in, qkv_flat, preferred_element_type=jnp.float32).astype(jnp.bfloat16)
    packed = packed.reshape(img_group, TILE, heads_here, 3, head_size)
    queries = packed[:, :, :, 0, :]
    keys_part = packed[:, :, :, 1, :]
    values_part = packed[:, :, :, 2, :]
    scaling = 1.0 / head_size**0.5
    scores = (
        jnp.einsum("gqhd,gkhd->ghqk", queries, keys_part, preferred_element_type=jnp.float32)
        * scaling
    )
    same_kind = (live_tiles[:, :, None] == live_tiles[:, None, :])[:, None]
    scores = jnp.where(same_kind, scores, -1e30)
    row_max = jnp.max(scores, axis=-1, keepdims=True)
    exp_terms = jnp.exp(scores - row_max)
    probability = exp_terms / jnp.sum(exp_terms, axis=-1, keepdims=True)
    prob_low = probability.astype(jnp.bfloat16)
    mixed = jnp.einsum(
        "ghqk,gkhd->gqhd", prob_low, values_part, preferred_element_type=jnp.float32
    ).astype(jnp.bfloat16)
    mixed = mixed.reshape(rows_here, heads_here * head_size)
    middle_b = vis_grad.astype(jnp.bfloat16)
    out_term = dot_tn(mixed, middle_b)
    mixed_grad = (
        dot_nt(middle_b, w_out).astype(jnp.bfloat16).reshape(img_group, TILE, heads_here, head_size)
    )
    prob_grad = jnp.einsum(
        "gqhd,gkhd->ghqk", mixed_grad, values_part, preferred_element_type=jnp.float32
    )
    score_grad = (
        probability
        * (prob_grad - jnp.sum(probability * prob_grad, axis=-1, keepdims=True))
        * scaling
    )
    score_grad = score_grad.astype(jnp.bfloat16)
    q_grad = jnp.einsum(
        "ghqk,gkhd->gqhd", score_grad, keys_part, preferred_element_type=jnp.float32
    )
    k_grad = jnp.einsum("ghqk,gqhd->gkhd", score_grad, queries, preferred_element_type=jnp.float32)
    v_grad = jnp.einsum("ghqk,gqhd->gkhd", prob_low, mixed_grad, preferred_element_type=jnp.float32)
    packed_grad = jnp.stack([q_grad, k_grad, v_grad], axis=3).astype(jnp.bfloat16)
    packed_grad = packed_grad.reshape(rows_here, heads_here * 3 * head_size)
    qkv_term = dot_tn(normed_in, packed_grad).reshape(features_dim, heads_here, 3 * head_size)
    in_part = dot_nt(packed_grad, qkv_flat)
    share_width = features_dim // lax.axis_size("tp")
    share_start = tp_rank * share_width
    in_sum = lax.psum(in_part.astype(jnp.bfloat16), "tp").astype(jnp.float32)
    in_back, ln1_term = norm_back(in_sum, normed1, inverse1, ln1_gain)
    grad_full = (vis_grad + in_back).astype(jnp.bfloat16)
    grad_input = lax.dynamic_slice_in_dim(grad_full, share_start, share_width, 1)
    grad_proj, grad_qkv, grad_out, grad_ln1 = (
        lax.psum_scatter(
            proj_term.astype(jnp.bfloat16), "enc", scatter_dimension=0, tiled=True
        ).astype(jnp.float32),
        lax.psum_scatter(
            qkv_term.astype(jnp.bfloat16), "enc", scatter_dimension=0, tiled=True
        ).astype(jnp.float32),
        lax.psum_scatter(
            out_term.astype(jnp.bfloat16), "enc", scatter_dimension=1, tiled=True
        ).astype(jnp.float32),
        lax.psum_scatter(
            ln1_term.astype(jnp.bfloat16), "enc", scatter_dimension=0, tiled=True
        ).astype(jnp.float32),
    )
    return (grad_input, grad_proj, grad_qkv, grad_out, grad_ln1)


def solution(mesh):
    placed = (
        P("enc", "tp"),
        P("enc", None),
        P("enc", "tp"),
        P(),
        P(),
        P(),
        P(None, "tp", None),
        P("tp", None),
        P(None, "tp"),
    )
    return jax.shard_map(
        shards,
        mesh=mesh,
        in_specs=placed,
        out_specs=(P("enc", "tp"), P("enc", "tp"), P("enc", "tp", None), P("tp", "enc"), P("enc")),
        check_vma=False,
    )
```

profile of v0, /device:TPU:0, one launch (start us, length us, event | category | flops | bytes accessed | tf_op | source)
XLA Modules:
  0.0 404.1 jit_solution(6433689965465876006)
XLA Ops:
  7.2 7.0 %convolution_convert_fusion.4 = bf16[384,1280]{0,1:T(8,128)(2,1)} fusion(bf16[384,2048]{1,0:T(8,128)(2,1)} %param.11, bf16[1280,2048]{1,0:T(8,128)(2,1)} %param.19), kind=kOutput, calls=%fused_computation.10 | convolution fusion | flops 2013757440 | bytes 7798784 | tf_op jit(solution)/shard_map/dot_general | solution.py:33
  14.6 11.6 %all_gather.7 = bf16[384,1280]{0,1:T(8,128)(2,1)} all-gather(bf16[384,320]{0,1:T(8,128)(2,1)S(1)} %copy-done.5), channel_id=1, replica_groups=mesh['enc'=8,'tp'=4] {'tp'}, dimensions={1}, use_global_device_ids=true | all-gather | bytes 1228800 | tf_op jit(solution)/shard_map/all_gather | solution.py:50
  29.7 2.5 convolution_convert_fusion.5
  32.2 3.2 reshape.234
  35.9 5.7 %reduce-scatter.5.cloned.1.call-done = bf16[384,320]{0,1:T(8,128)(2,1)} async-done(((bf16[384,1280]{0,1:T(8,128)(2,1)}), bf16[384,320]{0,1:T(8,128)(2,1)}) %reduce-scatter.5.cloned.1.call-update) | async-done | bytes 245776 | tf_op jit(solution)/shard_map/reduce_scatter | solution.py:75
  48.7 2.7 scatter_fusion
  53.7 5.5 %all-to-all-start = ((bf16[8,128,320]{1,2,0:T(8,128)(2,1)}), bf16[8,128,320]{1,2,0:T(8,128)(2,1)}, u32[]{:S(2)}, u32[]{:S(2)}) async-start(bf16[8,128,320]{1,2,0:T(8,128)(2,1)} %convert_element_type.112), calls=%async_computation.1 | async-start | bytes 1310720 | tf_op jit(solution)/shard_map/all_to_all | solution.py:78
  59.5 2.4 fusion.52
  61.9 2.4 fusion.53
  64.3 12.2 %all-to-all-done = bf16[8,128,320]{1,2,0:T(8,128)(2,1)} async-done(((bf16[8,128,320]{1,2,0:T(8,128)(2,1)}), bf16[8,128,320]{1,2,0:T(8,128)(2,1)}, u32[]{:S(2)}, u32[]{:S(2)}) %all-to-all-start) | async-done | bytes 655392 | tf_op jit(solution)/shard_map/all_to_all | solution.py:78
  76.5 2.4 gather_fusion
  83.4 8.7 %all_gather.6 = bf16[384,1280]{0,1:T(8,128)(2,1)S(1)} all-gather(bf16[384,320]{0,1:T(8,128)(2,1)S(1)} %select_convert_fusion), channel_id=1, replica_groups=mesh['enc'=8,'tp'=4] {'tp'}, dimensions={1}, use_global_device_ids=true | all-gather | bytes 1228800 | tf_op jit(solution)/shard_map/all_gather | solution.py:81
  93.2 2.4 convolution_convert_fusion.6
  99.7 2.3 convolution_bitcast_fusion
  102.0 3.1 convolution_bitcast_fusion.2
  105.1 3.1 convolution_bitcast_fusion.1
  117.3 4.4 %convolution_convert_fusion.1 = bf16[1280,4,240]{2,0,1:T(8,128)(2,1)} fusion(bf16[4,240,384]{2,1,0:T(8,128)(2,1)} %bitcast.97, f32[1280]{0:T(1024)S(1)} %copy-done.7, bf16[384,1280]{1,0:T(8,128)(2,1)S(1)} %copy.120, f32[384]{0:T(512)S(1)} %add_rsqrt_fusion, f32[384]{0:T(512)S(1)} %broadcast_multiply_fusion.2), kind=kOutput, calls=%fused_computation.7 | convolution fusion | flops 947404800 | bytes 4186112 | tf_op jit(solution)/shard_map/dot_general | solution.py:39
  121.8 7.1 %convolution_convert_fusion = bf16[1280,2048]{1,0:T(8,128)(2,1)} fusion(bf16[384,2048]{1,0:T(8,128)(2,1)} %param.11, bf16[384,1280]{1,0:T(8,128)(2,1)} %param.12, pred[384]{0:T(512)(128)(4,1)S(1)} %get-tuple-element.44), kind=kOutput, calls=%fused_computation.6 | convolution fusion | flops 2016378880 | bytes 7799168 | tf_op jit(solution)/shard_map/dot_general | solution.py:39
  134.3 14.2 %all-reduce.3.cloned.1.call-done = bf16[384,1280]{1,0:T(8,128)(2,1)} async-done(((bf16[384,1280]{1,0:T(8,128)(2,1)}), bf16[384,1280]{1,0:T(8,128)(2,1)}) %all-reduce.3.cloned.1.call-update) | async-done | bytes 983056 | tf_op jit(solution)/shard_map/psum | solution.py:141
  152.2 21.4 %all-reduce = bf16[1280]{0:T(1024)(128)(2,1)S(1)} all-reduce(bf16[1280]{0:T(1024)(128)(2,1)S(1)} %get-tuple-element.36), channel_id=6, replica_groups=mesh['enc'=8,'tp'=4] {'enc'}, use_global_device_ids=true, to_apply=%region_18.20.clone | all-reduce | flops 1280 | bytes 5120
  174.2 42.1 %reduce-scatter.11.cloned.1.call-done = bf16[320,160]{0,1:T(8,128)(2,1)} async-done(((bf16[320,1280]{0,1:T(8,128)(2,1)}), bf16[320,160]{0,1:T(8,128)(2,1)}) %reduce-scatter.11.cloned.1.call-update) | async-done | bytes 102416 | tf_op jit(solution)/shard_map/reduce_scatter | solution.py:152
  217.9 71.7 %reduce-scatter.9.cloned.1.call-done = bf16[160,4,240]{2,0,1:T(8,128)(2,1)} async-done(((bf16[1280,4,240]{2,0,1:T(8,128)(2,1)}), bf16[160,4,240]{2,0,1:T(8,128)(2,1)}) %reduce-scatter.9.cloned.1.call-update) | async-done | bytes 307216 | tf_op jit(solution)/shard_map/reduce_scatter | solution.py:149
  291.7 103.6 %reduce-scatter.7.cloned.1.call-done = bf16[160,2048]{1,0:T(8,128)(2,1)} async-done(((bf16[1280,2048]{1,0:T(8,128)(2,1)}), bf16[160,2048]{1,0:T(8,128)(2,1)}) %reduce-scatter.7.cloned.1.call-update) | async-done | bytes 655376 | tf_op jit(solution)/shard_map/reduce_scatter | solution.py:146
  395.3 2.3 convert_element_type.128
  (84 shorter events, 45.5 us)
Async XLA Ops:
  7.2 22.6 %copy-start = (bf16[1280,4,240]{0,2,1:T(8,128)(2,1)S(1)}, bf16[1280,4,240]{0,2,1:T(8,128)(2,1)}, u32[]{:S(2)}) copy-start(bf16[1280,4,240]{0,2,1:T(8,128)(2,1)} %param.17) | copy-start | bytes 7372804
  7.2 7.1 %copy-start.6 = (s32[8,3]{0,1:T(4,128)S(1)}, s32[8,3]{0,1:T(4,128)}, u32[]{:S(2)}) copy-start(s32[8,3]{0,1:T(4,128)} %param.15) | copy-start | bytes 292
  7.2 7.4 %copy-start.5 = (bf16[384,320]{0,1:T(8,128)(2,1)S(1)}, bf16[384,320]{0,1:T(8,128)(2,1)}, u32[]{:S(2)}) copy-start(bf16[384,320]{0,1:T(8,128)(2,1)} %param.13) | copy-start | bytes 737284
  7.2 34.4 %reduce-scatter.5.cloned.1.call-start = ((), (), s32[]{:S(2)}) async-start(), calls=%async_computation.5 | async-start | bytes 1228800 | tf_op jit(solution)/shard_map/reduce_scatter | solution.py:75
  14.6 13.5 %copy-start.8 = (s32[8,3]{0,1:T(4,128)S(1)}, s32[8,3]{0,1:T(4,128)}, u32[]{:S(2)}) copy-start(s32[8,3]{0,1:T(4,128)} %param.14) | copy-start | bytes 292
  26.2 3.5 copy-start.7
  53.7 22.8 %all-to-all-start = ((bf16[8,128,320]{1,2,0:T(8,128)(2,1)}), bf16[8,128,320]{1,2,0:T(8,128)(2,1)}, u32[]{:S(2)}, u32[]{:S(2)}) async-start(bf16[8,128,320]{1,2,0:T(8,128)(2,1)} %convert_element_type.112), calls=%async_computation.1 | async-start | bytes 1310720 | tf_op jit(solution)/shard_map/all_to_all | solution.py:78
  59.2 89.3 %all-reduce.3.cloned.1.call-start = ((), (), s32[]{:S(2)}) async-start(), calls=%async_computation.6 | async-start | bytes 1966080 | tf_op jit(solution)/shard_map/psum | solution.py:141
  92.2 1.1 copy-start.1
  110.3 0.9 copy-start.3
  113.4 102.9 %reduce-scatter.11.cloned.1.call-start = ((), (), s32[]{:S(2)}) async-start(), calls=%async_computation.9 | async-start | bytes 1105920 | tf_op jit(solution)/shard_map/reduce_scatter | solution.py:152
  113.6 1.8 copy-start.2
  117.3 172.4 %reduce-scatter.9.cloned.1.call-start = ((), (), s32[]{:S(2)}) async-start(), calls=%async_computation.8 | async-start | bytes 2949120 | tf_op jit(solution)/shard_map/reduce_scatter | solution.py:149
  121.8 273.5 %reduce-scatter.7.cloned.1.call-start = ((), (), s32[]{:S(2)}) async-start(), calls=%async_computation.7 | async-start | bytes 5898240 | tf_op jit(solution)/shard_map/reduce_scatter | solution.py:146
  128.9 0.7 copy-start.9
  148.5 2.3 copy-start.4
Sparse Core Ops, SparseCore 0:
  14.4 27.1 reduce-scatter.4
  113.5 34.9 all-reduce.2
  151.8 64.4 reduce-scatter.10
  219.7 69.9 reduce-scatter.8
  293.1 102.1 reduce-scatter.6
where the time goes:
time: 405 us; the launch traced here: 404 us
  waiting for transfers between devices  250 us (62%)
  matrix products  42.2 us (10%)
  blocking collectives  41.7 us (10%)
  local copies, waits for them, and re-layouts  34.8 us (9%)
  other arithmetic  15.3 us (4%)
  between operations  14.7 us (4%)
  starting transfers between devices  5.9 us (1%)
    reduce_scatter x1, waiting for transfers between devices, shards(): lax.psum_scatter(proj_term.astype(jnp.bfloat16), 'enc', scatter_dimension...  104 us
    reduce_scatter x1, waiting for transfers between devices, shards(): lax.psum_scatter(qkv_term.astype(jnp.bfloat16), 'enc', scatter_dimension=...  71.7 us
    reduce_scatter x1, waiting for transfers between devices, shards(): lax.psum_scatter(out_term.astype(jnp.bfloat16), 'enc', scatter_dimension=...  42.1 us
    unnamed x1, blocking collectives  21.4 us
    psum x1, waiting for transfers between devices, shards(): in_sum = lax.psum(in_part.astype(jnp.bfloat16), 'tp').astype(jnp.float32)  14.2 us
    dot_general x3, matrix products, dot_tn(): lax.dot_general(left, right, (((0,), (0,)), ((), ())), preferred_element_...  13.2 us
    all_to_all x1, waiting for transfers between devices, shards(): lax.all_to_all(outgoing(shared).astype(jnp.bfloat16), 'enc', split_axis=0...  12.2 us
    all_gather x1, blocking collectives, shards(): block_full = lax.all_gather(block_in, 'tp', axis=1, tiled=True)  11.6 us
  transfers between devices with their start and end apart: 6, of which 6 were waited for; matrix products, arithmetic and copies ran while one was open for 10% of the time, Pallas kernels for 0%

commit v1 on v0

--- a/solution.py
+++ b/solution.py
@@ -138,7 +138,9 @@
     in_part = dot_nt(packed_grad, qkv_flat)
     share_width = features_dim // lax.axis_size("tp")
     share_start = tp_rank * share_width
-    in_sum = lax.psum(in_part.astype(jnp.bfloat16), "tp").astype(jnp.float32)
+    in_sum = (
+        lax.all_gather(in_part.astype(jnp.bfloat16), axis_name="tp").sum(axis=0).astype(jnp.float32)
+    )
     in_back, ln1_term = norm_back(in_sum, normed1, inverse1, ln1_gain)
     grad_full = (vis_grad + in_back).astype(jnp.bfloat16)
     grad_input = lax.dynamic_slice_in_dim(grad_full, share_start, share_width, 1)

time: 405 us -> 383 us (0.946)
  waiting for transfers between devices: 250 us -> 223 us
    all_gather x0 -> x1, waiting for transfers between devices: none -> 31.5 us  [shards(): lax.all_gather(in_part.astype(jnp.bfloat16), axis_name='tp').sum(axis=0)]
    reduce_scatter x1, waiting for transfers between devices: 104 us -> 76.2 us  [shards(): lax.psum_scatter(proj_term.astype(jnp.bfloat16), 'enc', scatter_dimension...]
    reduce_scatter x1, waiting for transfers between devices: 42.1 us -> 27.4 us  [shards(): lax.psum_scatter(out_term.astype(jnp.bfloat16), 'enc', scatter_dimension=...]
    psum x1 -> x0, waiting for transfers between devices: 14.2 us -> none  [shards(): in_sum = lax.psum(in_part.astype(jnp.bfloat16), 'tp').astype(jnp.float32)]
    unnamed x27 -> x29, local copies, waits for them, and re-layouts: 8.21 us -> 8.11 us
  transfers between devices with their start and end apart: 6 -> 6, of which waited for: 6 -> 6; matrix products, arithmetic and copies ran while one was open for 10% -> 16% of each run, Pallas kernels for 0% -> 0%
where the time goes in v1:
time: 383 us; the launch traced here: 382 us
  waiting for transfers between devices  223 us (58%)
  matrix products  42.6 us (11%)
  blocking collectives  42.5 us (11%)
  local copies, waits for them, and re-layouts  35.4 us (9%)
  other arithmetic  18 us (5%)
  between operations  14.7 us (4%)
  starting transfers between devices  5.89 us (2%)
    reduce_scatter x1, waiting for transfers between devices, shards(): lax.psum_scatter(proj_term.astype(jnp.bfloat16), 'enc', scatter_dimension...  76.2 us
    reduce_scatter x1, waiting for transfers between devices, shards(): lax.psum_scatter(qkv_term.astype(jnp.bfloat16), 'enc', scatter_dimension=...  72 us
    all_gather x1, waiting for transfers between devices, shards(): lax.all_gather(in_part.astype(jnp.bfloat16), axis_name='tp').sum(axis=0)  31.5 us
    reduce_scatter x1, waiting for transfers between devices, shards(): lax.psum_scatter(out_term.astype(jnp.bfloat16), 'enc', scatter_dimension=...  27.4 us
    unnamed x1, blocking collectives  22.2 us
    dot_general x3, matrix products, dot_nt(): lax.dot_general(left, right, (((1,), (1,)), ((), ())), preferred_element_...  13 us
    dot_general x3, matrix products, dot_tn(): lax.dot_general(left, right, (((0,), (0,)), ((), ())), preferred_element_...  13 us
    all_to_all x1, waiting for transfers between devices, shards(): lax.all_to_all(outgoing(shared).astype(jnp.bfloat16), 'enc', split_axis=0...  12.1 us
  transfers between devices with their start and end apart: 6, of which 6 were waited for; matrix products, arithmetic and copies ran while one was open for 16% of the time, Pallas kernels for 0%

profile of v1, /device:TPU:0, one launch (start us, length us, event | category | flops | bytes accessed | tf_op | source)
XLA Modules:
  0.0 381.7 jit_solution(17743417379007356578)
XLA Ops:
  7.3 7.0 %convolution_convert_fusion.4 = bf16[384,1280]{0,1:T(8,128)(2,1)} fusion(bf16[384,2048]{1,0:T(8,128)(2,1)} %param.11, bf16[1280,2048]{1,0:T(8,128)(2,1)} %param.19), kind=kOutput, calls=%fused_computation.10 | convolution fusion | flops 2013757440 | bytes 7798784 | tf_op jit(solution)/shard_map/dot_general | solution.py:33
  14.8 11.6 %all_gather.13 = bf16[384,1280]{0,1:T(8,128)(2,1)} all-gather(bf16[384,320]{0,1:T(8,128)(2,1)S(1)} %copy-done.4), channel_id=1, replica_groups=mesh['enc'=8,'tp'=4] {'tp'}, dimensions={1}, use_global_device_ids=true | all-gather | bytes 1228800 | tf_op jit(solution)/shard_map/all_gather | solution.py:50
  29.7 2.5 convolution_convert_fusion.5
  32.2 3.2 reshape.234
  35.9 2.4 fusion.52
  38.3 3.2 reduce-scatter.5.cloned.1.call-done
  48.7 2.7 scatter_fusion
  53.6 5.5 %all-to-all-start = ((bf16[8,128,320]{1,2,0:T(8,128)(2,1)}), bf16[8,128,320]{1,2,0:T(8,128)(2,1)}, u32[]{:S(2)}, u32[]{:S(2)}) async-start(bf16[8,128,320]{1,2,0:T(8,128)(2,1)} %convert_element_type.114), calls=%async_computation.1 | async-start | bytes 1310720 | tf_op jit(solution)/shard_map/all_to_all | solution.py:78
  59.3 2.4 fusion.53
  64.3 12.1 %all-to-all-done = bf16[8,128,320]{1,2,0:T(8,128)(2,1)} async-done(((bf16[8,128,320]{1,2,0:T(8,128)(2,1)}), bf16[8,128,320]{1,2,0:T(8,128)(2,1)}, u32[]{:S(2)}, u32[]{:S(2)}) %all-to-all-start) | async-done | bytes 655392 | tf_op jit(solution)/shard_map/all_to_all | solution.py:78
  83.4 8.7 %all_gather.12 = bf16[384,1280]{0,1:T(8,128)(2,1)S(1)} all-gather(bf16[384,320]{0,1:T(8,128)(2,1)S(1)} %select_convert_fusion), channel_id=1, replica_groups=mesh['enc'=8,'tp'=4] {'tp'}, dimensions={1}, use_global_device_ids=true | all-gather | bytes 1228800 | tf_op jit(solution)/shard_map/all_gather | solution.py:81
  93.0 2.7 convolution_convert_fusion.2
  96.0 2.7 convolution_convert_fusion.6
  102.8 3.1 convolution_bitcast_fusion.2
  105.9 3.1 convolution_bitcast_fusion.1
  112.4 3.3 convolution_convert_fusion.1
  115.7 3.3 convolution_convert_fusion.3
  119.2 7.0 %convolution_convert_fusion = bf16[1280,2048]{1,0:T(8,128)(2,1)} fusion(bf16[384,2048]{1,0:T(8,128)(2,1)} %param.11, bf16[384,1280]{1,0:T(8,128)(2,1)} %param.12, pred[384]{0:T(512)(128)(4,1)S(1)} %get-tuple-element.44), kind=kOutput, calls=%fused_computation.6 | convolution fusion | flops 2016378880 | bytes 7799168 | tf_op jit(solution)/shard_map/dot_general | solution.py:39
  131.6 27.4 %reduce-scatter.11.cloned.1.call-done = bf16[320,160]{0,1:T(8,128)(2,1)} async-done(((bf16[320,1280]{0,1:T(8,128)(2,1)}), bf16[320,160]{0,1:T(8,128)(2,1)}) %reduce-scatter.11.cloned.1.call-update) | async-done | bytes 102416 | tf_op jit(solution)/shard_map/reduce_scatter | solution.py:154
  160.6 72.0 %reduce-scatter.9.cloned.1.call-done = bf16[160,4,240]{2,0,1:T(8,128)(2,1)} async-done(((bf16[1280,4,240]{2,0,1:T(8,128)(2,1)}), bf16[160,4,240]{2,0,1:T(8,128)(2,1)}) %reduce-scatter.9.cloned.1.call-update) | async-done | bytes 307216 | tf_op jit(solution)/shard_map/reduce_scatter | solution.py:151
  234.7 31.5 %all-gather.3.cloned.1.call-done = bf16[1536,1280]{1,0:T(8,128)(2,1)} async-done(((bf16[384,1280]{1,0:T(8,128)(2,1)}), bf16[1536,1280]{1,0:T(8,128)(2,1)}) %all-gather.3.cloned.1.call-update) | async-done | bytes 3932176 | tf_op jit(solution)/shard_map/all_gather | solution.py:142
  266.2 3.9 %reduce_sum.102 = bf16[384,1280]{1,0:T(8,128)(2,1)} reduce(bf16[4,384,1280]{2,1,0:T(8,128)(2,1)} %bitcast.96, bf16[]{:T(256)} %constant.70.clone.1), dimensions={0}, to_apply=%region_11.13 | reduce | flops 1474560 | bytes 4915202 | tf_op jit(solution)/shard_map/reduce_sum | solution.py:142
  273.8 22.2 %all-reduce = bf16[1280]{0:T(1024)(128)(2,1)S(1)} all-reduce(bf16[1280]{0:T(1024)(128)(2,1)S(1)} %get-tuple-element.36), channel_id=7, replica_groups=mesh['enc'=8,'tp'=4] {'enc'}, use_global_device_ids=true, to_apply=%region_18.20.clone | all-reduce | flops 1280 | bytes 5120
  296.6 76.2 %reduce-scatter.7.cloned.1.call-done = bf16[160,2048]{1,0:T(8,128)(2,1)} async-done(((bf16[1280,2048]{1,0:T(8,128)(2,1)}), bf16[160,2048]{1,0:T(8,128)(2,1)}) %reduce-scatter.7.cloned.1.call-update) | async-done | bytes 655376 | tf_op jit(solution)/shard_map/reduce_scatter | solution.py:148
  (87 shorter events, 47.3 us)
Async XLA Ops:
  7.2 22.5 %copy-start = (bf16[1280,4,240]{0,2,1:T(8,128)(2,1)S(1)}, bf16[1280,4,240]{0,2,1:T(8,128)(2,1)}, u32[]{:S(2)}) copy-start(bf16[1280,4,240]{0,2,1:T(8,128)(2,1)} %param.17) | copy-start | bytes 7372804
  7.2 7.1 %copy-start.7 = (s32[8,3]{0,1:T(4,128)S(1)}, s32[8,3]{0,1:T(4,128)}, u32[]{:S(2)}) copy-start(s32[8,3]{0,1:T(4,128)} %param.15) | copy-start | bytes 292
  7.2 7.5 %copy-start.9 = (s32[8,3]{0,1:T(4,128)S(1)}, s32[8,3]{0,1:T(4,128)}, u32[]{:S(2)}) copy-start(s32[8,3]{0,1:T(4,128)} %param.14) | copy-start | bytes 292
  7.2 7.6 %copy-start.4 = (bf16[384,320]{0,1:T(8,128)(2,1)S(1)}, bf16[384,320]{0,1:T(8,128)(2,1)}, u32[]{:S(2)}) copy-start(bf16[384,320]{0,1:T(8,128)(2,1)} %param.13) | copy-start | bytes 737284
  7.2 34.3 %reduce-scatter.5.cloned.1.call-start = ((), (), s32[]{:S(2)}) async-start(), calls=%async_computation.5 | async-start | bytes 1228800 | tf_op jit(solution)/shard_map/reduce_scatter | solution.py:75
  26.4 3.3 copy-start.8
  53.6 22.8 %all-to-all-start = ((bf16[8,128,320]{1,2,0:T(8,128)(2,1)}), bf16[8,128,320]{1,2,0:T(8,128)(2,1)}, u32[]{:S(2)}, u32[]{:S(2)}) async-start(bf16[8,128,320]{1,2,0:T(8,128)(2,1)} %convert_element_type.114), calls=%async_computation.1 | async-start | bytes 1310720 | tf_op jit(solution)/shard_map/all_to_all | solution.py:78
  59.2 99.9 %reduce-scatter.11.cloned.1.call-start = ((), (), s32[]{:S(2)}) async-start(), calls=%async_computation.8 | async-start | bytes 1105920 | tf_op jit(solution)/shard_map/reduce_scatter | solution.py:154
  92.1 0.9 copy-start.1
  95.8 136.8 %reduce-scatter.9.cloned.1.call-start = ((), (), s32[]{:S(2)}) async-start(), calls=%async_computation.7 | async-start | bytes 2949120 | tf_op jit(solution)/shard_map/reduce_scatter | solution.py:151
  109.0 1.7 copy-start.5
  109.0 1.7 copy-start.6
  111.5 0.9 copy-start.2
  115.7 150.5 %all-gather.3.cloned.1.call-start = ((), (), s32[]{:S(2)}) async-start(), calls=%async_computation.9 | async-start | bytes 4915200 | tf_op jit(solution)/shard_map/all_gather | solution.py:142
  119.1 253.7 %reduce-scatter.7.cloned.1.call-start = ((), (), s32[]{:S(2)}) async-start(), calls=%async_computation.6 | async-start | bytes 5898240 | tf_op jit(solution)/shard_map/reduce_scatter | solution.py:148
  126.2 0.7 copy-start.10
  270.1 2.3 copy-start.3
Sparse Core Ops, SparseCore 0:
  14.4 27.1 reduce-scatter.4
  95.9 63.0 reduce-scatter.10
  162.6 69.9 reduce-scatter.8
  234.0 32.1 all-gather.2
  269.6 103.2 reduce-scatter.6
